TPU v7x, 256 devices: a whole 4x4x8 slice. The times are simulated.
256 devices in a mesh: clip: 32 (over z_lo, y, core), row: 2 (over z_hi), src: 4 (over x).
Axes of the slice: x: 4, y: 4, z: 8 (z_hi: 2, z_lo: 4; z = z_hi * 4 + z_lo), core: 2. Of those that a mesh axis runs over, the one named last changes fastest.
Arguments:
- mask_clip: bfloat16 [131072, 4096], P(('clip', 'row'), 'src'), parts along dimension 0, may hold values from -6 to 6
- source_shifts: int32 [16, 2], P('src'), may hold values from -64 to 64
- source_weights: int32 [16], P('src'), may hold values from 1 to 8
Outputs:
- intensity: float32 [32768, 1024], P(('clip', 'row', 'src')), parts along dimension 0
There are 32 independent parts, one for each index of `clip`. A program takes and returns all parts, laid end to end along the dimension named above; an argument that names none is the same for every part. Nothing has to cross between parts.
All inputs are finite; a program needn't handle non-finite values.
Results may differ from a plain program's by a relative error of at most 0.0052.
Values may be sent and summed in bfloat16 or wider, within the bound.
No kernel may reach another device: no remote copies, remote signals or barrier semaphores. Data moves between devices by JAX's collectives and lax.ppermute only.
A program may use at most 64 MiB of HBM per device.

v0:
```python
import math
import jax
import jax.numpy as jnp
from jax import lax
from jax.sharding import PartitionSpec as P

NM = 4096
P_SIZE = 256
NI = 1024


def twiddles(positions, length, scaling):
    frequency = jnp.arange(P_SIZE, dtype=jnp.int32) - P_SIZE // 2
    product = jnp.mod(positions[:, None] * frequency[None, :], length)
    angles = product.astype(jnp.float32) * jnp.float32(2.0 * math.pi / length)
    return (jnp.cos(angles) * jnp.float32(scaling), jnp.sin(angles) * jnp.float32(scaling))


def tile_spectrum(mask_tile, row_first, col_first):
    row_index = row_first + jnp.arange(mask_tile.shape[0], dtype=jnp.int32)
    col_index = col_first + jnp.arange(mask_tile.shape[1], dtype=jnp.int32)
    col_cos, col_sin = twiddles(col_index, NM, 1.0 / math.sqrt(NM))
    col_table = jnp.concatenate([col_cos, -col_sin], 1).astype(jnp.bfloat16)
    half_way = jnp.dot(mask_tile, col_table, preferred_element_type=jnp.float32).astype(
        jnp.bfloat16
    )
    row_cos, row_sin = twiddles(row_index, NM, 1.0 / math.sqrt(NM))
    row_table = jnp.concatenate([row_cos, row_sin], 1).T.astype(jnp.bfloat16)
    blocks = jnp.dot(row_table, half_way, preferred_element_type=jnp.float32)
    real_part = blocks[:P_SIZE, :P_SIZE] + blocks[P_SIZE:, P_SIZE:]
    imag_part = blocks[:P_SIZE, P_SIZE:] - blocks[P_SIZE:, :P_SIZE]
    return jnp.stack([real_part, imag_part])


def build_left(image_rows):
    row_cos, row_sin = twiddles(image_rows, NI, 1.0 / math.sqrt(P_SIZE))
    return jnp.concatenate([row_cos, row_sin], 0).astype(jnp.bfloat16)


def build_right():
    col_cos, col_sin = twiddles(jnp.arange(NI, dtype=jnp.int32), NI, 1.0 / math.sqrt(P_SIZE))
    upper = jnp.concatenate([col_cos.T, col_sin.T], 1)
    lower = jnp.concatenate([-col_sin.T, col_cos.T], 1)
    return jnp.concatenate([upper, lower], 0).astype(jnp.bfloat16)


def source_image(spectrum, shift_pair, weight, left_table, right_table):
    frequency = jnp.arange(P_SIZE, dtype=jnp.int32) - P_SIZE // 2
    along_rows = frequency + shift_pair[0]
    along_cols = frequency + shift_pair[1]
    radius = P_SIZE // 4
    inside = (
        along_rows[:, None] * along_rows[:, None] + along_cols[None, :] * along_cols[None, :]
        <= radius * radius
    )
    pupil_mask = inside.astype(jnp.bfloat16)
    passed = jnp.concatenate([spectrum[0] * pupil_mask, spectrum[1] * pupil_mask], 1)
    blocks = jnp.dot(left_table, passed, preferred_element_type=jnp.float32)
    row_count = left_table.shape[0] // 2
    k_real = blocks[:row_count, :P_SIZE] - blocks[row_count:, P_SIZE:]
    k_imag = blocks[:row_count, P_SIZE:] + blocks[row_count:, :P_SIZE]
    partial_value = jnp.concatenate([k_real, k_imag], 1).astype(jnp.bfloat16)
    field_pair = jnp.dot(partial_value, right_table, preferred_element_type=jnp.float32)
    field_real = field_pair[:, :NI]
    field_imag = field_pair[:, NI:]
    return weight.astype(jnp.float32) * (field_real * field_real + field_imag * field_imag)


def image_rows_sum(spectrum, image_rows, all_shifts, all_weights, right_table):
    left_table = build_left(image_rows)

    def add_source(running, source_item):
        shift_pair, weight = source_item
        return (running + source_image(spectrum, shift_pair, weight, left_table, right_table), None)

    summed, _ = lax.scan(
        add_source, jnp.zeros((image_rows.shape[0], NI), jnp.float32), (all_shifts, all_weights)
    )
    return summed


def body(mask_clip, source_shifts, source_weights):
    row_id = lax.axis_index("row")
    src_id = lax.axis_index("src")
    strip_rows = mask_clip.shape[0]
    strip_cols = mask_clip.shape[1]
    partial_value = tile_spectrum(mask_clip, row_id * strip_rows, src_id * strip_cols)
    spectrum = lax.psum(partial_value, ("row", "src")).astype(jnp.bfloat16)
    right_table = build_right()
    image_strip = NI // lax.axis_size("row")
    rows_dev = image_strip // lax.axis_size("src")
    sources = source_shifts.shape[0] * lax.axis_size("src")
    image_rows = row_id * image_strip + jnp.arange(rows_dev * lax.axis_size("src"), dtype=jnp.int32)
    summed = lax.psum_scatter(
        image_rows_sum(spectrum, image_rows, source_shifts, source_weights, right_table),
        "src",
        scatter_dimension=0,
        tiled=True,
    )
    return summed / jnp.float32(sources)


def solution(mesh):
    placed = (P(("clip", "row"), "src"), P("src", None), P("src"))
    return jax.shard_map(
        body, mesh=mesh, in_specs=placed, out_specs=P(("clip", "row", "src"), None), check_vma=False
    )
```

profile of v0, /device:TPU:1, one launch (start us, length us, event | category | flops | bytes accessed | tf_op | source)
XLA Modules:
  0.0 177.1 jit_solution(12008709048086519349)
XLA Ops:
  6.6 5.7 %fusion.35 = (bf16[256,1024]{1,0:T(8,128)(2,1)S(1)}, bf16[256,1024]{1,0:T(8,128)(2,1)}, bf16[256,1024]{1,0:T(8,128)(2,1)}) fusion(s32[256]{0:T(256)S(1)} %iota_add_fusion.4), kind=kLoop, calls=%fused_computation.70 | loop fusion | flops 5242880 | bytes 1573888 | tf_op jit(solution)/shard_map/convert.7
  12.3 3.2 %multiply_convert_fusion.5 = (bf16[512,256]{1,0:T(8,128)(2,1)}, bf16[512,256]{1,0:T(8,128)(2,1)}) fusion(s32[256]{0:T(256)S(1)} %iota_add_fusion.4, s32[512]{0:T(512)S(1)} %iota_add_fusion.3), kind=kLoop, calls=%fused_computation.79 | loop fusion | flops 2359296 | bytes 527360 | tf_op jit(solution)/shard_map/convert.8
  15.5 5.6 %multiply_convert_fusion.3 = (bf16[1024,256]{1,0:T(8,128)(2,1)S(1)}, bf16[1024,256]{1,0:T(8,128)(2,1)}) fusion(s32[256]{0:T(256)S(1)} %iota_add_fusion.4, s32[1024]{0:T(1024)S(1)} %iota_add_fusion.2), kind=kLoop, calls=%fused_computation.65 | loop fusion | flops 4980736 | bytes 1053696 | tf_op jit(solution)/shard_map/convert.10
  21.1 10.2 %multiply_convert_fusion.1 = (bf16[2048,256]{1,0:T(8,128)(2,1)}, bf16[2048,256]{1,0:T(8,128)(2,1)}) fusion(s32[256]{0:T(256)S(1)} %iota_add_fusion.4, s32[2048]{0:T(1024)S(1)} %iota_add_fusion.1), kind=kLoop, calls=%fused_computation.41 | loop fusion | flops 9437184 | bytes 2106368 | tf_op jit(solution)/shard_map/convert.12
  31.3 7.5 %fusion.19 = f32[512,512]{1,0:T(8,128)} fusion(bf16[2048,256]{1,0:T(8,128)(2,1)} %get-tuple-element.144, bf16[2048,256]{1,0:T(8,128)(2,1)} %get-tuple-element.143, bf16[2048,1024]{1,0:T(8,128)(2,1)} %param.5, bf16[1024,256]{1,0:T(8,128)(2,1)} %get-tuple-element.146, bf16[1024,256]{1,0:T(8,128)(2,1)S(1)} %get-tuple-element.145), kind=kOutput, calls=%fused_computation.35 | convolution fusion | flops 3228565504 | bytes 8388608 | tf_op jit(solution)/shard_map/dot_general | solution.py:29
  38.8 1.3 fusion.42
  40.1 63.6 %all-reduce.1 = bf16[2,256,256]{2,1,0:T(8,128)(2,1)S(1)} all-reduce(f32[2,256,256]{2,1,0:T(8,128)S(1)} %pad_maximum_fusion), channel_id=1, replica_groups=mesh['clip'=32,'row'=2,'src'=4] {'row','src'}, use_global_device_ids=true, to_apply=%region_0.1 | all-reduce | flops 131072 | bytes 786432 | tf_op jit(solution)/shard_map/psum | solution.py:88
  103.7 1.1 pad_maximum_fusion.1
  104.8 2.9 %maximum_maximum_fusion = bf16[512,2048]{1,0:T(8,128)(2,1)} fusion(bf16[256,1024]{1,0:T(8,128)(2,1)} %get-tuple-element.151, bf16[256,1024]{1,0:T(8,128)(2,1)} %get-tuple-element.150, bf16[256,1024]{1,0:T(8,128)(2,1)S(1)} %get-tuple-element.149), kind=kLoop, calls=%fused_computation.39 | loop fusion | flops 8388608 | bytes 3670016 | tf_op jit(solution)/shard_map/concatenate | solution.py:44
  107.7 29.0 %while.13 = (s32[]{:T(128)}, f32[512,1024]{1,0:T(8,128)S(1)}, s32[4]{0:T(128)S(1)}, s32[4,2]{0,1:T(2,128)S(1)}, bf16[2,256,256]{2,1,0:T(8,128)(2,1)S(1)}, /*inde...) while((s32[]{:T(128)}, f32[512,1024]{1,0:T(8,128)S(1)}, ...), condition=%wide.region_2.3_spmd.clone, body=%wide.region_1.2_spmd.clone.sunk | while | flops 1347683584 | bytes 29626572 | solution.py:76
  109.5 1.2 add_multiply_fusion.3
  111.5 0.9 copy-done.1
  112.5 1.3 fusion.65
  113.8 1.2 fusion.66
  115.0 0.6 dynamic_slice.20
  116.8 1.2 add_multiply_fusion.3
  118.8 0.9 copy-done.1
  119.7 1.3 fusion.65
  121.0 1.2 fusion.66
  122.2 0.6 dynamic_slice.20
  124.1 1.2 add_multiply_fusion.3
  126.1 0.9 copy-done.1
  127.0 1.3 fusion.65
  128.3 1.2 fusion.66
  129.5 0.6 dynamic_slice.20
  131.3 1.2 add_multiply_fusion.3
  133.3 0.9 copy-done.1
  134.3 1.3 fusion.65
  135.6 1.2 fusion.66
  136.8 1.3 copy-done
  138.1 30.2 %reduce-scatter.2.cloned.1.call-done = f32[128,1024]{1,0:T(8,128)} async-done(((f32[512,1024]{1,0:T(8,128)}), f32[128,1024]{1,0:T(8,128)}) %reduce-scatter.2.cloned.1.call-update) | async-done | bytes 524304 | tf_op jit(solution)/shard_map/reduce_scatter | solution.py:94
  168.3 1.9 %broadcast_multiply_fusion = f32[128,1024]{1,0:T(8,128)} fusion(f32[128,1024]{1,0:T(8,128)} %reduce-scatter.2.cloned.1.call-done), kind=kLoop, calls=%fused_computation.84 | loop fusion | flops 131072 | bytes 1048576 | tf_op jit(solution)/shard_map/div | solution.py:100
  (38 shorter events, 6.1 us)
Async XLA Ops:
  6.5 161.8 %reduce-scatter.2.cloned.1.call-start = ((), (), s32[]{:S(2)}) async-start(), calls=%async_computation.1 | async-start | bytes 2621440 | tf_op jit(solution)/shard_map/reduce_scatter | solution.py:94
  104.8 2.9 %copy-start.2 = (s32[4,2]{0,1:T(2,128)S(1)}, s32[4,2]{0,1:T(2,128)}, u32[]{:S(2)}) copy-start(s32[4,2]{0,1:T(2,128)} %param.6) | copy-start | bytes 100
  104.8 2.9 %copy-start.3 = (s32[4]{0:T(128)S(1)}, s32[4]{0:T(128)}, u32[]{:S(2)}) copy-start(s32[4]{0:T(128)} %param.7) | copy-start | bytes 52
  110.9 1.6 copy-start.1
  118.1 1.6 copy-start.1
  125.4 1.6 copy-start.1
  132.7 1.6 copy-start.1
  136.8 1.3 copy-start
Sparse Core Ops, SparseCore 0:
  138.2 30.0 reduce-scatter.1
where the time goes:
time: 178 us; the launch traced here: 177 us
  blocking collectives  63.6 us (36%)
  other arithmetic  42.6 us (24%)
  waiting for transfers between devices  30.2 us (17%)
  matrix products  14.5 us (8%)
  between operations  13.5 us (8%)
  local copies, waits for them, and re-layouts  9.76 us (5%)
  loops' own time  2.82 us (2%)
    psum x1, blocking collectives, body(): spectrum = lax.psum(partial_value, ('row', 'src')).astype(jnp.bfloat16)  63.6 us
    reduce_scatter x1, waiting for transfers between devices, body(): lax.psum_scatter(image_rows_sum(spectrum, image_rows, source_shifts, sour...  30.2 us
    another operation x8, other arithmetic  25.4 us
    dot_general x1, matrix products, tile_spectrum(): blocks = jnp.dot(row_table, half_way, preferred_element_type=jnp.float32)  7.46 us
    dot_general x4, matrix products, source_image(): jnp.dot(partial_value, right_table, preferred_element_type=jnp.float32)  5.14 us
    add x4, other arithmetic, add_source(): running + source_image(spectrum, shift_pair, weight, left_table, right_ta...  4.83 us
    mul x4, other arithmetic, source_image(): along_cols[None, :] * along_cols[None, :]  4.79 us
    while x8, local copies, waits for them, and re-layouts  3.71 us
  transfers between devices with their start and end apart: 1, of which 1 were waited for; matrix products, arithmetic and copies ran while one was open for 0% of the time, Pallas kernels for 0%

commit v1 on v0

--- a/solution.py
+++ b/solution.py
@@ -7,6 +7,11 @@
 NM = 4096
 P_SIZE = 256
 NI = 1024
+
+
+def gather_and_add(value, axis):
+    parts = lax.all_gather(value, axis)
+    return jnp.sum(parts, axis=0)
 
 
 def twiddles(positions, length, scaling):
@@ -85,7 +90,7 @@
     strip_rows = mask_clip.shape[0]
     strip_cols = mask_clip.shape[1]
     partial_value = tile_spectrum(mask_clip, row_id * strip_rows, src_id * strip_cols)
-    spectrum = lax.psum(partial_value, ("row", "src")).astype(jnp.bfloat16)
+    spectrum = gather_and_add(partial_value, ("row", "src")).astype(jnp.bfloat16)
     right_table = build_right()
     image_strip = NI // lax.axis_size("row")
     rows_dev = image_strip // lax.axis_size("src")

time: 178 us -> 209 us (1.17)
  waiting for transfers between devices: 30.2 us -> 129 us
  blocking collectives: 63.6 us -> 0 us
  other arithmetic: 42.6 us -> 40.5 us
    all_gather x0 -> x1, waiting for transfers between devices: none -> 101 us  [gather_and_add(): parts = lax.all_gather(value, axis)]
    psum x1 -> x0, blocking collectives: 63.6 us -> none  [body(): spectrum = lax.psum(partial_value, ('row', 'src')).astype(jnp.bfloat16)]
    reduce_scatter x1, waiting for transfers between devices: 30.2 us -> 27.7 us  [body(): lax.psum_scatter(image_rows_sum(spectrum, image_rows, source_shifts, sour...]
    reduce_sum x0 -> x1, other arithmetic: none -> 2.51 us  [gather_and_add(): return jnp.sum(parts, axis=0)]
  transfers between devices with their start and end apart: 1 -> 2, of which waited for: 1 -> 2; matrix products, arithmetic and copies ran while one was open for 0% -> 4% of each run, Pallas kernels for 0% -> 0%
where the time goes in v1:
time: 209 us
  waiting for transfers between devices  129 us (62%)
  other arithmetic  40.5 us (19%)
  between operations  13.5 us (6%)
  matrix products  13.1 us (6%)
  local copies, waits for them, and re-layouts  10 us (5%)
  loops' own time  2.83 us (1%)
    all_gather x1, waiting for transfers between devices, gather_and_add(): parts = lax.all_gather(value, axis)  101 us
    reduce_scatter x1, waiting for transfers between devices, body(): lax.psum_scatter(image_rows_sum(spectrum, image_rows, source_shifts, sour...  27.7 us
    another operation x8, other arithmetic  23.3 us
    dot_general x1, matrix products, tile_spectrum(): blocks = jnp.dot(row_table, half_way, preferred_element_type=jnp.float32)  5.99 us
    dot_general x4, matrix products, source_image(): jnp.dot(partial_value, right_table, preferred_element_type=jnp.float32)  5.14 us
    mul x4, other arithmetic, source_image(): along_cols[None, :] * along_cols[None, :]  5.08 us
    add x4, other arithmetic, add_source(): running + source_image(spectrum, shift_pair, weight, left_table, right_ta...  4.83 us
  transfers between devices with their start and end apart: 2, of which 2 were waited for; matrix products, arithmetic and copies ran while one was open for 4% of the time, Pallas kernels for 0%

profile of v1, /device:TPU:1, one launch (start us, length us, event | category | flops | bytes accessed | tf_op | source)
XLA Modules:
  0.0 208.9 jit_solution(8015263370144460074)
XLA Ops:
  6.5 5.7 %multiply_convert_fusion.3 = (bf16[1024,256]{1,0:T(8,128)(2,1)}, bf16[1024,256]{1,0:T(8,128)(2,1)}) fusion(s32[256]{0:T(256)S(1)} %iota_add_fusion.4, s32[1024]{0:T(1024)S(1)} %iota_add_fusion.2), kind=kLoop, calls=%fused_computation.65 | loop fusion | flops 4980736 | bytes 1053696 | tf_op jit(solution)/shard_map/convert.10
  12.3 9.5 %multiply_convert_fusion.1 = (bf16[2048,256]{1,0:T(8,128)(2,1)S(1)}, bf16[2048,256]{1,0:T(8,128)(2,1)S(1)}) fusion(s32[256]{0:T(256)S(1)} %iota_add_fusion.4, s32[2048]{0:T(1024)S(1)} %iota_add_fusion.1), kind=kLoop, calls=%fused_computation.41 | loop fusion | flops 9437184 | bytes 2106368 | tf_op jit(solution)/shard_map/convert.12
  21.8 6.0 %fusion.19 = f32[512,512]{1,0:T(8,128)S(1)} fusion(bf16[2048,256]{1,0:T(8,128)(2,1)S(1)} %get-tuple-element.144, bf16[2048,256]{1,0:T(8,128)(2,1)S(1)} %get-tuple-element.143, bf16[2048,1024]{1,0:T(8,128)(2,1)} %param.5, bf16[1024,256]{1,0:T(8,128)(2,1)} %get-tuple-element.146, bf16[1024,256]{1,0:T(8,128)(2,1)} %get-tuple-element.145), kind=kOutput, calls=%fused_computation.35 | convolution fusion | flops 3228565504 | bytes 8388608 | tf_op jit(solution)/shard_map/dot_general | solution.py:34
  27.8 0.8 pad_maximum_fusion
  28.8 2.5 %multiply_convert_fusion.5 = (bf16[512,256]{1,0:T(8,128)(2,1)S(1)}, bf16[512,256]{1,0:T(8,128)(2,1)S(1)}) fusion(s32[256]{0:T(256)S(1)} %iota_add_fusion.4, s32[512]{0:T(512)S(1)} %iota_add_fusion.3), kind=kLoop, calls=%fused_computation.79 | loop fusion | flops 2359296 | bytes 527360 | tf_op jit(solution)/shard_map/convert.8
  31.3 4.9 %fusion.35 = (bf16[256,1024]{1,0:T(8,128)(2,1)S(1)}, bf16[256,1024]{1,0:T(8,128)(2,1)S(1)}, bf16[256,1024]{1,0:T(8,128)(2,1)S(1)}) fusion(s32[256]{0:T(256)S(1)} %iota_add_fusion.4), kind=kLoop, calls=%fused_computation.70 | loop fusion | flops 5242880 | bytes 1573888 | tf_op jit(solution)/shard_map/convert.7
  36.3 1.5 maximum_maximum_fusion
  37.8 101.2 %all-gather.3.cloned.1.call-done = f32[16,256,256]{2,1,0:T(8,128)} async-done(((f32[2,256,256]{2,1,0:T(8,128)}), f32[16,256,256]{2,1,0:T(8,128)}) %all-gather.3.cloned.1.call-update) | async-done | bytes 4194320 | tf_op jit(solution)/shard_map/all_gather | solution.py:13
  139.0 2.5 %reduce_sum.9 = bf16[2,256,256]{2,1,0:T(8,128)(2,1)S(1)} reduce(f32[8,2,256,256]{3,2,1,0:T(8,128)} %bitcast.31, f32[]{:T(128)} %constant.94.clone.1), dimensions={0}, to_apply=%region_0.1 | reduce | flops 917504 | bytes 4456452 | tf_op jit(solution)/shard_map/reduce_sum | solution.py:14
  141.5 29.6 %while.13 = (s32[]{:T(128)}, f32[512,1024]{1,0:T(8,128)S(1)}, s32[4]{0:T(128)S(1)}, s32[4,2]{0,1:T(2,128)S(1)}, bf16[2,256,256]{2,1,0:T(8,128)(2,1)S(1)}, /*inde...) while((s32[]{:T(128)}, f32[512,1024]{1,0:T(8,128)S(1)}, ...), condition=%wide.region_2.3_spmd.clone, body=%wide.region_1.2_spmd.clone.sunk | while | flops 1347683584 | bytes 29626572 | solution.py:81
  141.5 0.6 dynamic_slice.20
  143.4 1.3 add_multiply_fusion.3
  145.5 0.9 copy-done.1
  146.4 1.3 fusion.65
  147.7 1.2 fusion.66
  148.9 0.6 dynamic_slice.20
  150.8 1.3 add_multiply_fusion.3
  152.9 0.9 copy-done.1
  153.8 1.3 fusion.65
  155.1 1.2 fusion.66
  156.3 0.6 dynamic_slice.20
  158.2 1.3 add_multiply_fusion.3
  160.3 0.9 copy-done.1
  161.2 1.3 fusion.65
  162.5 1.2 fusion.66
  165.6 1.3 add_multiply_fusion.3
  167.7 0.9 copy-done.1
  168.6 1.3 fusion.65
  169.9 1.2 fusion.66
  171.1 1.3 copy-done
  172.5 27.7 %reduce-scatter.2.cloned.1.call-done = f32[128,1024]{1,0:T(8,128)} async-done(((f32[512,1024]{1,0:T(8,128)}), f32[128,1024]{1,0:T(8,128)}) %reduce-scatter.2.cloned.1.call-update) | async-done | bytes 524304 | tf_op jit(solution)/shard_map/reduce_scatter | solution.py:99
  200.2 1.9 broadcast_multiply_fusion
  (41 shorter events, 6.5 us)
Async XLA Ops:
  6.5 132.4 %all-gather.3.cloned.1.call-start = ((), (), s32[]{:S(2)}) async-start(), calls=%async_computation.2 | async-start | bytes 4718592 | tf_op jit(solution)/shard_map/all_gather | solution.py:13
  28.7 171.5 %reduce-scatter.2.cloned.1.call-start = ((), (), s32[]{:S(2)}) async-start(), calls=%async_computation.1 | async-start | bytes 2621440 | tf_op jit(solution)/shard_map/reduce_scatter | solution.py:99
  139.0 2.5 %copy-start.2 = (s32[4,2]{0,1:T(2,128)S(1)}, s32[4,2]{0,1:T(2,128)}, u32[]{:S(2)}) copy-start(s32[4,2]{0,1:T(2,128)} %param.6) | copy-start | bytes 100
  139.0 2.5 %copy-start.3 = (s32[4]{0:T(128)S(1)}, s32[4]{0:T(128)}, u32[]{:S(2)}) copy-start(s32[4]{0:T(128)} %param.7) | copy-start | bytes 52
  144.8 1.6 copy-start.1
  152.2 1.6 copy-start.1
  159.6 1.6 copy-start.1
  167.0 1.6 copy-start.1
  171.1 1.3 copy-start
Sparse Core Ops, SparseCore 0:
  28.8 110.1 all-gather.2
  172.6 27.5 reduce-scatter.1
